TPU v7x, 32 devices: a whole 2x2x4 slice. The times are simulated.
32 devices in a mesh: gx: 4 (over z), gy: 4 (over x, core), gz: 2 (over y).
Axes of the slice: x: 2, y: 2, z: 4, core: 2. Of those that a mesh axis runs over, the one named last changes fastest.
Arguments:
- blocks: bfloat16 [4, 4, 128, 256, 256], P('gy', 'gx'), may hold values from -0.0625 to 0.0625
- block_rows: int32 [4, 4, 128], P('gy', 'gx'), may hold values from 0 to 15
- block_cols: int32 [4, 4, 128], P('gy', 'gx'), may hold values from 0 to 15
- probe_bits: int32 [16384, 256], P(('gy', 'gx'), 'gz'), may hold values from 0 to 1
- shift: float32 [16384], P(('gy', 'gx')), may hold values from 0 to 0.7
Outputs:
- forms: float32 [3, 256], P(None, 'gz')
- last_term: float32 [16384, 256], P(('gy', 'gx'), 'gz')
All inputs are finite; a program needn't handle non-finite values.
Results may differ from a plain program's by a relative error of at most 0.02.
Values may be sent and summed in bfloat16 or wider, within the bound.
No kernel may reach another device: no remote copies, remote signals or barrier semaphores. Data moves between devices by JAX's collectives and lax.ppermute only.
A program may use at most 128 MiB of HBM per device.

v0:
```python
import jax
import jax.numpy as jnp
from jax import lax
from jax.sharding import PartitionSpec as P


def body(blocks, block_rows, block_cols, probe_bits, shift):
    tile_blocks = blocks[0, 0]
    rows_here = block_rows[0, 0]
    cols_here = block_cols[0, 0]
    block_size = tile_blocks.shape[1]
    local_rows = shift.shape[0]
    probe_count = probe_bits.shape[1]
    tile_rows = local_rows // block_size * lax.axis_size("gx")
    signs = (2 * probe_bits - 1).astype(jnp.float32)

    def apply_operator(field):
        rounded = field.astype(jnp.bfloat16)
        whole = lax.all_gather(rounded, "gy", axis=0, tiled=True)
        whole = whole.reshape(whole.shape[0] // block_size, block_size, probe_count)
        picked = whole[cols_here]
        product = jnp.einsum(
            "kab,kbp->kap", tile_blocks, picked, preferred_element_type=jnp.float32
        )
        partial_rows = (
            jnp.zeros((tile_rows, block_size, probe_count), jnp.float32).at[rows_here].add(product)
        )
        summed = lax.psum_scatter(
            partial_rows.reshape(lax.axis_size("gx") * local_rows, probe_count).astype(
                jnp.bfloat16
            ),
            "gx",
            scatter_dimension=0,
            tiled=True,
        ).astype(jnp.float32)
        return summed + shift[:, None] * field

    first = apply_operator(signs)
    second = 2.0 * apply_operator(first) - signs
    third = 2.0 * apply_operator(second) - first
    forms = jnp.stack(
        [lax.psum(jnp.sum(signs * term, axis=0), ("gx", "gy")) for term in (first, second, third)]
    )
    return (forms, third)


def solution(mesh):
    return jax.shard_map(
        body,
        mesh=mesh,
        in_specs=(
            P("gy", "gx", None, None, None),
            P("gy", "gx", None),
            P("gy", "gx", None),
            P(("gy", "gx"), "gz"),
            P(("gy", "gx")),
        ),
        out_specs=(P(None, "gz"), P(("gy", "gx"), "gz")),
        check_vma=False,
    )
```

profile of v0, /device:TPU:0, one launch (start us, length us, event | category | flops | bytes accessed | tf_op | source)
XLA Modules:
  0.0 390.7 jit_solution(4236453247020909070)
XLA Ops:
  7.2 1.8 convert_convert_fusion
  10.4 19.1 %all-gather.4.cloned.1.call-done = bf16[4096,128]{1,0:T(8,128)(2,1)} async-done(((bf16[1024,128]{1,0:T(8,128)(2,1)}), bf16[4096,128]{1,0:T(8,128)(2,1)}) %all-gather.4.cloned.1.call-update) | async-done | bytes 1048592 | tf_op jit(solution)/shard_map/all_gather | solution.py:19
  29.6 7.8 %gather_fusion = bf16[128,256,128]{2,1,0:T(8,128)(2,1)} fusion(bf16[16,256,128]{2,1,0:T(8,128)(2,1)} %bitcast.39, s32[1024]{0:T(1024)S(1)} %pad_clamp_fusion), kind=kCustom, calls=%fused_computation | custom fusion | bytes 16777728 | tf_op jit(solution)/shard_map/gather | solution.py:21
  37.3 17.2 %fusion.6 = f32[128,256,128]{1,2,0:T(8,128)} fusion(bf16[128,256,128]{2,1,0:T(8,128)(2,1)} %gather_fusion, bf16[1,1,128,256,256]{4,3,2,1,0:T(8,128)(2,1)} %param.5), kind=kOutput, calls=%fused_computation.12 | convolution fusion | flops 2147483648 | bytes 41943040 | tf_op jit(solution)/shard_map/kab,kbp->kap/dot_general | solution.py:22
  54.5 17.4 %copy.11 = f32[128,256,128]{2,1,0:T(8,128)} copy(f32[128,256,128]{1,2,0:T(8,128)} %fusion.6) | data formatting | bytes 33554432 | tf_op jit(solution)/shard_map/kab,kbp->kap/dot_general | solution.py:22
  72.1 24.3 %scatter_fusion = f32[16,256,128]{2,1,0:T(8,128)S(1)} fusion(f32[16,256,128]{2,1,0:T(8,128)S(1)} %broadcast.45.clone, s32[128]{0:T(128)S(1)} %fusion.17, f32[128,256,128]{2,1,0:T(8,128)} %copy.11), kind=kCustom, calls=%fused_computation.3 | custom fusion | flops 4194304 | bytes 50332160 | tf_op jit(solution)/shard_map/scatter-add | solution.py:26
  96.5 1.2 convert_element_type.41
  97.7 27.4 %reduce-scatter.4.cloned.1.call-done = bf16[1024,128]{1,0:T(8,128)(2,1)} async-done(((bf16[4096,128]{1,0:T(8,128)(2,1)}), bf16[1024,128]{1,0:T(8,128)(2,1)}) %reduce-scatter.4.cloned.1.call-update) | async-done | bytes 262160 | tf_op jit(solution)/shard_map/reduce_scatter | solution.py:28
  125.1 1.9 fusion.15
  127.0 15.5 %all-gather.6.cloned.1.call-done = bf16[4096,128]{1,0:T(8,128)(2,1)} async-done(((bf16[1024,128]{1,0:T(8,128)(2,1)}), bf16[4096,128]{1,0:T(8,128)(2,1)}) %all-gather.6.cloned.1.call-update) | async-done | bytes 1048592 | tf_op jit(solution)/shard_map/all_gather | solution.py:19
  142.5 7.8 %gather_fusion.1 = bf16[128,256,128]{2,1,0:T(8,128)(2,1)} fusion(bf16[16,256,128]{2,1,0:T(8,128)(2,1)} %bitcast.41, s32[1024]{0:T(1024)S(1)} %pad_clamp_fusion), kind=kCustom, calls=%fused_computation.1 | custom fusion | bytes 16777728 | tf_op jit(solution)/shard_map/gather | solution.py:21
  150.3 17.2 %fusion.9 = f32[128,256,128]{1,2,0:T(8,128)} fusion(bf16[128,256,128]{2,1,0:T(8,128)(2,1)} %gather_fusion.1, bf16[1,1,128,256,256]{4,3,2,1,0:T(8,128)(2,1)} %param.5), kind=kOutput, calls=%fused_computation.13 | convolution fusion | flops 2147483648 | bytes 41943040 | tf_op jit(solution)/shard_map/kab,kbp->kap/dot_general | solution.py:22
  167.4 17.4 %copy.13 = f32[128,256,128]{2,1,0:T(8,128)} copy(f32[128,256,128]{1,2,0:T(8,128)} %fusion.9) | data formatting | bytes 33554432 | tf_op jit(solution)/shard_map/kab,kbp->kap/dot_general | solution.py:22
  185.1 24.3 %scatter_fusion.1 = f32[16,256,128]{2,1,0:T(8,128)S(1)} fusion(f32[16,256,128]{2,1,0:T(8,128)S(1)} %broadcast.45.clone.1, s32[128]{0:T(128)S(1)} %fusion.17, f32[128,256,128]{2,1,0:T(8,128)} %copy.13), kind=kCustom, calls=%fused_computation.4 | custom fusion | flops 4194304 | bytes 50332160 | tf_op jit(solution)/shard_map/scatter-add | solution.py:26
  210.6 27.4 %reduce-scatter.6.cloned.1.call-done = bf16[1024,128]{1,0:T(8,128)(2,1)} async-done(((bf16[4096,128]{1,0:T(8,128)(2,1)}), bf16[1024,128]{1,0:T(8,128)(2,1)}) %reduce-scatter.6.cloned.1.call-update) | async-done | bytes 262160 | tf_op jit(solution)/shard_map/reduce_scatter | solution.py:28
  238.0 1.9 fusion.16
  240.2 15.1 %all-gather.8.cloned.1.call-done = bf16[4096,128]{1,0:T(8,128)(2,1)} async-done(((bf16[1024,128]{1,0:T(8,128)(2,1)}), bf16[4096,128]{1,0:T(8,128)(2,1)}) %all-gather.8.cloned.1.call-update) | async-done | bytes 1048592 | tf_op jit(solution)/shard_map/all_gather | solution.py:19
  255.3 7.8 %gather_fusion.2 = bf16[128,256,128]{2,1,0:T(8,128)(2,1)} fusion(bf16[16,256,128]{2,1,0:T(8,128)(2,1)} %bitcast.40, s32[1024]{0:T(1024)S(1)} %pad_clamp_fusion), kind=kCustom, calls=%fused_computation.2 | custom fusion | bytes 16777728 | tf_op jit(solution)/shard_map/gather | solution.py:21
  263.1 17.2 %fusion.12 = f32[128,256,128]{1,2,0:T(8,128)} fusion(bf16[128,256,128]{2,1,0:T(8,128)(2,1)} %gather_fusion.2, bf16[1,1,128,256,256]{4,3,2,1,0:T(8,128)(2,1)} %param.5), kind=kOutput, calls=%fused_computation.14 | convolution fusion | flops 2147483648 | bytes 41943040 | tf_op jit(solution)/shard_map/kab,kbp->kap/dot_general | solution.py:22
  280.3 17.4 %copy.15 = f32[128,256,128]{2,1,0:T(8,128)} copy(f32[128,256,128]{1,2,0:T(8,128)} %fusion.12) | data formatting | bytes 33554432 | tf_op jit(solution)/shard_map/kab,kbp->kap/dot_general | solution.py:22
  297.9 24.3 %scatter_fusion.2 = f32[16,256,128]{2,1,0:T(8,128)S(1)} fusion(f32[16,256,128]{2,1,0:T(8,128)S(1)} %broadcast.45, s32[128]{0:T(128)S(1)} %fusion.17, f32[128,256,128]{2,1,0:T(8,128)} %copy.15), kind=kCustom, calls=%fused_computation.5 | custom fusion | flops 4194304 | bytes 50332160 | tf_op jit(solution)/shard_map/scatter-add | solution.py:26
  323.4 27.4 %reduce-scatter.8.cloned.1.call-done = bf16[1024,128]{1,0:T(8,128)(2,1)} async-done(((bf16[4096,128]{1,0:T(8,128)(2,1)}), bf16[1024,128]{1,0:T(8,128)(2,1)}) %reduce-scatter.8.cloned.1.call-update) | async-done | bytes 262160 | tf_op jit(solution)/shard_map/reduce_scatter | solution.py:28
  350.9 2.2 multiply_reduce_fusion.2
  353.0 30.2 %all-reduce = (f32[1,128]{1,0:T(1,128)S(1)}, f32[1,128]{1,0:T(1,128)S(1)}, f32[1,128]{1,0:T(1,128)S(1)}) all-reduce(f32[1,128]{1,0:T(1,128)S(1)} %bitcast.47, f32[1,128]{1,0:T(1,128)S(1)} %bitcast.46, f32[1,128]{1,0:T(1,128)S(1)} %bitcast.45), channel_id=1, replica_groups=mesh['gx'=4,'gy'=4,'gz'=2] {'gx','gy'}, use_global_device_ids=true, to_apply=%region_11.0 | all-reduce | flops 384 | bytes 3072 | tf_op jit(solution)/shard_map/psum | solution.py:42
  (29 shorter events, 5.4 us)
Async XLA Ops:
  7.2 22.4 %all-gather.4.cloned.1.call-start = ((), (), s32[]{:S(2)}) async-start(), calls=%async_computation.3 | async-start | bytes 1310720 | tf_op jit(solution)/shard_map/all_gather | solution.py:19
  9.1 116.0 %reduce-scatter.4.cloned.1.call-start = ((), (), s32[]{:S(2)}) async-start(), calls=%async_computation.4 | async-start | bytes 1310720 | tf_op jit(solution)/shard_map/reduce_scatter | solution.py:28
  72.1 53.0 %copy-start = (s32[1024,128]{1,0:T(8,128)S(1)}, s32[1024,128]{1,0:T(8,128)}, u32[]{:S(2)}) copy-start(s32[1024,128]{1,0:T(8,128)} %param.8) | copy-start | bytes 1572868
  72.1 53.0 %copy-start.3 = (f32[1024]{0:T(1024)S(1)}, f32[1024]{0:T(1024)}, u32[]{:S(2)}) copy-start(f32[1024]{0:T(1024)} %param.9) | copy-start | bytes 12292
  97.7 44.8 %all-gather.6.cloned.1.call-start = ((), (), s32[]{:S(2)}) async-start(), calls=%async_computation.5 | async-start | bytes 1310720 | tf_op jit(solution)/shard_map/all_gather | solution.py:19
  127.0 111.0 %reduce-scatter.6.cloned.1.call-start = ((), (), s32[]{:S(2)}) async-start(), calls=%async_computation.6 | async-start | bytes 1310720 | tf_op jit(solution)/shard_map/reduce_scatter | solution.py:28
  185.1 53.0 %copy-start.1 = (bf16[1024,128]{1,0:T(8,128)(2,1)S(1)}, bf16[1024,128]{1,0:T(8,128)(2,1)}, u32[]{:S(2)}) copy-start(bf16[1024,128]{1,0:T(8,128)(2,1)} %reduce-scatter.4.cloned.1.call-done) | copy-start | bytes 786436
  210.6 44.7 %all-gather.8.cloned.1.call-start = ((), (), s32[]{:S(2)}) async-start(), calls=%async_computation.7 | async-start | bytes 1310720 | tf_op jit(solution)/shard_map/all_gather | solution.py:19
  240.0 110.9 %reduce-scatter.8.cloned.1.call-start = ((), (), s32[]{:S(2)}) async-start(), calls=%async_computation.8 | async-start | bytes 1310720 | tf_op jit(solution)/shard_map/reduce_scatter | solution.py:28
  297.9 53.0 %copy-start.2 = (bf16[1024,128]{1,0:T(8,128)(2,1)S(1)}, bf16[1024,128]{1,0:T(8,128)(2,1)}, u32[]{:S(2)}) copy-start(bf16[1024,128]{1,0:T(8,128)(2,1)} %reduce-scatter.6.cloned.1.call-done) | copy-start | bytes 786436
Sparse Core Ops, SparseCore 0:
  10.1 19.4 all-gather.3
  97.8 27.2 reduce-scatter.3
  127.2 15.2 all-gather.5
  210.7 27.2 reduce-scatter.5
  240.1 15.1 all-gather.7
  323.6 27.2 reduce-scatter.7
where the time goes:
time: 393 us; the launch traced here: 391 us
  waiting for transfers between devices  132 us (34%)
  other arithmetic  86.2 us (22%)
  local copies, waits for them, and re-layouts  76.1 us (19%)
  matrix products  51.5 us (13%)
  blocking collectives  30.2 us (8%)
  between operations  14.2 us (4%)
    reduce_scatter x3, waiting for transfers between devices, apply_operator(): lax.psum_scatter(partial_rows.reshape(lax.axis_size('gx') * local_rows, p...  82.1 us
    scatter-add x3, other arithmetic, apply_operator(): jnp.zeros((tile_rows, block_size, probe_count), jnp.float32).at[rows_here]  73 us
    dot_general x3, local copies, waits for them, and re-layouts, apply_operator(): jnp.einsum('kab,kbp->kap', tile_blocks, picked, preferred_element_type=jn...  52.2 us
    dot_general x3, matrix products, apply_operator(): jnp.einsum('kab,kbp->kap', tile_blocks, picked, preferred_element_type=jn...  51.5 us
    all_gather x3, waiting for transfers between devices, apply_operator(): whole = lax.all_gather(rounded, 'gy', axis=0, tiled=True)  49.7 us
    psum x1, blocking collectives, body(): lax.psum(jnp.sum(signs * term, axis=0), ('gx', 'gy'))  30.2 us
    gather x3, local copies, waits for them, and re-layouts, apply_operator(): picked = whole[cols_here]  23.3 us
  transfers between devices with their start and end apart: 6, of which 6 were waited for; matrix products, arithmetic and copies ran while one was open for 0% of the time, Pallas kernels for 0%

commit v1 on v0

--- a/solution.py
+++ b/solution.py
@@ -39,7 +39,10 @@
     second = 2.0 * apply_operator(first) - signs
     third = 2.0 * apply_operator(second) - first
     forms = jnp.stack(
-        [lax.psum(jnp.sum(signs * term, axis=0), ("gx", "gy")) for term in (first, second, third)]
+        [
+            jnp.sum(lax.all_gather(jnp.sum(signs * term, axis=0), ("gx", "gy")), axis=0)
+            for term in (first, second, third)
+        ]
     )
     return (forms, third)
 

time: 393 us -> 418 us (1.064)
  blocking collectives: 30.2 us -> 55.1 us
    all_gather x0 -> x3, blocking collectives: none -> 55.1 us  [body(): lax.all_gather(jnp.sum(signs * term, axis=0), ('gx', 'gy'))]
    psum x1 -> x0, blocking collectives: 30.2 us -> none  [body(): lax.psum(jnp.sum(signs * term, axis=0), ('gx', 'gy'))]
where the time goes in v1:
time: 418 us; the launch traced here: 416 us
  waiting for transfers between devices  132 us (32%)
  other arithmetic  86.3 us (21%)
  local copies, waits for them, and re-layouts  76.1 us (18%)
  blocking collectives  55.1 us (13%)
  matrix products  51.5 us (12%)
  between operations  14.2 us (3%)
    reduce_scatter x3, waiting for transfers between devices, apply_operator(): lax.psum_scatter(partial_rows.reshape(lax.axis_size('gx') * local_rows, p...  82.1 us
    scatter-add x3, other arithmetic, apply_operator(): jnp.zeros((tile_rows, block_size, probe_count), jnp.float32).at[rows_here]  73 us
    all_gather x3, blocking collectives, body(): lax.all_gather(jnp.sum(signs * term, axis=0), ('gx', 'gy'))  55.1 us
    dot_general x3, local copies, waits for them, and re-layouts, apply_operator(): jnp.einsum('kab,kbp->kap', tile_blocks, picked, preferred_element_type=jn...  52.2 us
    dot_general x3, matrix products, apply_operator(): jnp.einsum('kab,kbp->kap', tile_blocks, picked, preferred_element_type=jn...  51.5 us
    all_gather x3, waiting for transfers between devices, apply_operator(): whole = lax.all_gather(rounded, 'gy', axis=0, tiled=True)  49.7 us
    gather x3, local copies, waits for them, and re-layouts, apply_operator(): picked = whole[cols_here]  23.3 us
  transfers between devices with their start and end apart: 6, of which 6 were waited for; matrix products, arithmetic and copies ran while one was open for 0% of the time, Pallas kernels for 0%

profile of v1, /device:TPU:0, one launch (start us, length us, event | category | flops | bytes accessed | tf_op | source)
XLA Modules:
  0.0 415.7 jit_solution(12632432343451279758)
XLA Ops:
  10.4 19.1 %all-gather.10.cloned.1.call-done = bf16[4096,128]{1,0:T(8,128)(2,1)} async-done(((bf16[1024,128]{1,0:T(8,128)(2,1)}), bf16[4096,128]{1,0:T(8,128)(2,1)}) %all-gather.10.cloned.1.call-update) | async-done | bytes 1048592 | tf_op jit(solution)/shard_map/all_gather | solution.py:19
  29.6 7.8 %gather_fusion = bf16[128,256,128]{2,1,0:T(8,128)(2,1)} fusion(bf16[16,256,128]{2,1,0:T(8,128)(2,1)} %bitcast.42, s32[1024]{0:T(1024)S(1)} %pad_clamp_fusion), kind=kCustom, calls=%fused_computation | custom fusion | bytes 16777728 | tf_op jit(solution)/shard_map/gather | solution.py:21
  37.3 17.2 %fusion.6 = f32[128,256,128]{1,2,0:T(8,128)} fusion(bf16[128,256,128]{2,1,0:T(8,128)(2,1)} %gather_fusion, bf16[1,1,128,256,256]{4,3,2,1,0:T(8,128)(2,1)} %param.5), kind=kOutput, calls=%fused_computation.12 | convolution fusion | flops 2147483648 | bytes 41943040 | tf_op jit(solution)/shard_map/kab,kbp->kap/dot_general | solution.py:22
  54.5 17.4 %copy.17 = f32[128,256,128]{2,1,0:T(8,128)} copy(f32[128,256,128]{1,2,0:T(8,128)} %fusion.6) | data formatting | bytes 33554432 | tf_op jit(solution)/shard_map/kab,kbp->kap/dot_general | solution.py:22
  72.1 24.3 %scatter_fusion = f32[16,256,128]{2,1,0:T(8,128)S(1)} fusion(f32[16,256,128]{2,1,0:T(8,128)S(1)} %broadcast.45.clone, s32[128]{0:T(128)S(1)} %fusion.17, f32[128,256,128]{2,1,0:T(8,128)} %copy.17), kind=kCustom, calls=%fused_computation.3 | custom fusion | flops 4194304 | bytes 50332160 | tf_op jit(solution)/shard_map/scatter-add | solution.py:26
  97.7 27.4 %reduce-scatter.4.cloned.1.call-done = bf16[1024,128]{1,0:T(8,128)(2,1)} async-done(((bf16[4096,128]{1,0:T(8,128)(2,1)}), bf16[1024,128]{1,0:T(8,128)(2,1)}) %reduce-scatter.4.cloned.1.call-update) | async-done | bytes 262160 | tf_op jit(solution)/shard_map/reduce_scatter | solution.py:28
  125.1 1.9 fusion.15
  127.0 15.5 %all-gather.12.cloned.1.call-done = bf16[4096,128]{1,0:T(8,128)(2,1)} async-done(((bf16[1024,128]{1,0:T(8,128)(2,1)}), bf16[4096,128]{1,0:T(8,128)(2,1)}) %all-gather.12.cloned.1.call-update) | async-done | bytes 1048592 | tf_op jit(solution)/shard_map/all_gather | solution.py:19
  142.5 7.8 %gather_fusion.1 = bf16[128,256,128]{2,1,0:T(8,128)(2,1)} fusion(bf16[16,256,128]{2,1,0:T(8,128)(2,1)} %bitcast.44, s32[1024]{0:T(1024)S(1)} %pad_clamp_fusion), kind=kCustom, calls=%fused_computation.1 | custom fusion | bytes 16777728 | tf_op jit(solution)/shard_map/gather | solution.py:21
  150.3 17.2 %fusion.9 = f32[128,256,128]{1,2,0:T(8,128)} fusion(bf16[128,256,128]{2,1,0:T(8,128)(2,1)} %gather_fusion.1, bf16[1,1,128,256,256]{4,3,2,1,0:T(8,128)(2,1)} %param.5), kind=kOutput, calls=%fused_computation.13 | convolution fusion | flops 2147483648 | bytes 41943040 | tf_op jit(solution)/shard_map/kab,kbp->kap/dot_general | solution.py:22
  167.4 17.4 %copy.19 = f32[128,256,128]{2,1,0:T(8,128)} copy(f32[128,256,128]{1,2,0:T(8,128)} %fusion.9) | data formatting | bytes 33554432 | tf_op jit(solution)/shard_map/kab,kbp->kap/dot_general | solution.py:22
  185.1 24.3 %scatter_fusion.1 = f32[16,256,128]{2,1,0:T(8,128)S(1)} fusion(f32[16,256,128]{2,1,0:T(8,128)S(1)} %broadcast.45.clone.1, s32[128]{0:T(128)S(1)} %fusion.17, f32[128,256,128]{2,1,0:T(8,128)} %copy.19), kind=kCustom, calls=%fused_computation.4 | custom fusion | flops 4194304 | bytes 50332160 | tf_op jit(solution)/shard_map/scatter-add | solution.py:26
  210.6 27.4 %reduce-scatter.6.cloned.1.call-done = bf16[1024,128]{1,0:T(8,128)(2,1)} async-done(((bf16[4096,128]{1,0:T(8,128)(2,1)}), bf16[1024,128]{1,0:T(8,128)(2,1)}) %reduce-scatter.6.cloned.1.call-update) | async-done | bytes 262160 | tf_op jit(solution)/shard_map/reduce_scatter | solution.py:28
  238.0 1.9 fusion.16
  240.2 15.1 %all-gather.14.cloned.1.call-done = bf16[4096,128]{1,0:T(8,128)(2,1)} async-done(((bf16[1024,128]{1,0:T(8,128)(2,1)}), bf16[4096,128]{1,0:T(8,128)(2,1)}) %all-gather.14.cloned.1.call-update) | async-done | bytes 1048592 | tf_op jit(solution)/shard_map/all_gather | solution.py:19
  255.3 7.8 %gather_fusion.2 = bf16[128,256,128]{2,1,0:T(8,128)(2,1)} fusion(bf16[16,256,128]{2,1,0:T(8,128)(2,1)} %bitcast.43, s32[1024]{0:T(1024)S(1)} %pad_clamp_fusion), kind=kCustom, calls=%fused_computation.2 | custom fusion | bytes 16777728 | tf_op jit(solution)/shard_map/gather | solution.py:21
  263.1 17.2 %fusion.12 = f32[128,256,128]{1,2,0:T(8,128)} fusion(bf16[128,256,128]{2,1,0:T(8,128)(2,1)} %gather_fusion.2, bf16[1,1,128,256,256]{4,3,2,1,0:T(8,128)(2,1)} %param.5), kind=kOutput, calls=%fused_computation.14 | convolution fusion | flops 2147483648 | bytes 41943040 | tf_op jit(solution)/shard_map/kab,kbp->kap/dot_general | solution.py:22
  280.3 17.4 %copy.21 = f32[128,256,128]{2,1,0:T(8,128)} copy(f32[128,256,128]{1,2,0:T(8,128)} %fusion.12) | data formatting | bytes 33554432 | tf_op jit(solution)/shard_map/kab,kbp->kap/dot_general | solution.py:22
  297.9 24.3 %scatter_fusion.2 = f32[16,256,128]{2,1,0:T(8,128)S(1)} fusion(f32[16,256,128]{2,1,0:T(8,128)S(1)} %broadcast.45, s32[128]{0:T(128)S(1)} %fusion.17, f32[128,256,128]{2,1,0:T(8,128)} %copy.21), kind=kCustom, calls=%fused_computation.5 | custom fusion | flops 4194304 | bytes 50332160 | tf_op jit(solution)/shard_map/scatter-add | solution.py:26
  323.4 27.4 %reduce-scatter.8.cloned.1.call-done = bf16[1024,128]{1,0:T(8,128)(2,1)} async-done(((bf16[4096,128]{1,0:T(8,128)(2,1)}), bf16[1024,128]{1,0:T(8,128)(2,1)}) %reduce-scatter.8.cloned.1.call-update) | async-done | bytes 262160 | tf_op jit(solution)/shard_map/reduce_scatter | solution.py:28
  350.9 2.2 multiply_reduce_fusion.2
  353.0 18.9 %all-gather.4 = f32[16,1,128]{2,1,0:T(1,128)S(1)} all-gather(f32[1,1,128]{2,1,0:T(1,128)S(1)} %bitcast.53), channel_id=3, replica_groups=mesh['gx'=4,'gy'=4,'gz'=2] {'gx','gy'}, dimensions={0}, use_global_device_ids=true | all-gather | bytes 8704 | tf_op jit(solution)/shard_map/all_gather | solution.py:43
  371.9 17.4 %all-gather.5 = f32[16,1,128]{2,1,0:T(1,128)S(1)} all-gather(f32[1,1,128]{2,1,0:T(1,128)S(1)} %bitcast.52), channel_id=4, replica_groups=mesh['gx'=4,'gy'=4,'gz'=2] {'gx','gy'}, dimensions={0}, use_global_device_ids=true | all-gather | bytes 8704 | tf_op jit(solution)/shard_map/all_gather | solution.py:43
  389.4 18.8 %all-gather.3 = f32[16,1,128]{2,1,0:T(1,128)S(1)} all-gather(f32[1,1,128]{2,1,0:T(1,128)S(1)} %bitcast.51), channel_id=2, replica_groups=mesh['gx'=4,'gy'=4,'gz'=2] {'gx','gy'}, dimensions={0}, use_global_device_ids=true | all-gather | bytes 8704 | tf_op jit(solution)/shard_map/all_gather | solution.py:43
  (34 shorter events, 8.5 us)
Async XLA Ops:
  7.2 22.4 %all-gather.10.cloned.1.call-start = ((), (), s32[]{:S(2)}) async-start(), calls=%async_computation.3 | async-start | bytes 1310720 | tf_op jit(solution)/shard_map/all_gather | solution.py:19
  9.1 116.0 %reduce-scatter.4.cloned.1.call-start = ((), (), s32[]{:S(2)}) async-start(), calls=%async_computation.4 | async-start | bytes 1310720 | tf_op jit(solution)/shard_map/reduce_scatter | solution.py:28
  72.1 53.0 %copy-start = (s32[1024,128]{1,0:T(8,128)S(1)}, s32[1024,128]{1,0:T(8,128)}, u32[]{:S(2)}) copy-start(s32[1024,128]{1,0:T(8,128)} %param.8) | copy-start | bytes 1572868
  72.1 53.0 %copy-start.3 = (f32[1024]{0:T(1024)S(1)}, f32[1024]{0:T(1024)}, u32[]{:S(2)}) copy-start(f32[1024]{0:T(1024)} %param.9) | copy-start | bytes 12292
  97.7 44.8 %all-gather.12.cloned.1.call-start = ((), (), s32[]{:S(2)}) async-start(), calls=%async_computation.5 | async-start | bytes 1310720 | tf_op jit(solution)/shard_map/all_gather | solution.py:19
  127.0 111.0 %reduce-scatter.6.cloned.1.call-start = ((), (), s32[]{:S(2)}) async-start(), calls=%async_computation.6 | async-start | bytes 1310720 | tf_op jit(solution)/shard_map/reduce_scatter | solution.py:28
  185.1 53.0 %copy-start.1 = (bf16[1024,128]{1,0:T(8,128)(2,1)S(1)}, bf16[1024,128]{1,0:T(8,128)(2,1)}, u32[]{:S(2)}) copy-start(bf16[1024,128]{1,0:T(8,128)(2,1)} %reduce-scatter.4.cloned.1.call-done) | copy-start | bytes 786436
  210.6 44.7 %all-gather.14.cloned.1.call-start = ((), (), s32[]{:S(2)}) async-start(), calls=%async_computation.7 | async-start | bytes 1310720 | tf_op jit(solution)/shard_map/all_gather | solution.py:19
  240.0 110.9 %reduce-scatter.8.cloned.1.call-start = ((), (), s32[]{:S(2)}) async-start(), calls=%async_computation.8 | async-start | bytes 1310720 | tf_op jit(solution)/shard_map/reduce_scatter | solution.py:28
  297.9 53.0 %copy-start.2 = (bf16[1024,128]{1,0:T(8,128)(2,1)S(1)}, bf16[1024,128]{1,0:T(8,128)(2,1)}, u32[]{:S(2)}) copy-start(bf16[1024,128]{1,0:T(8,128)(2,1)} %reduce-scatter.6.cloned.1.call-done) | copy-start | bytes 786436
Sparse Core Ops, SparseCore 0:
  10.1 19.4 all-gather.9
  97.8 27.2 reduce-scatter.3
  127.2 15.2 all-gather.11
  210.7 27.2 reduce-scatter.5
  240.1 15.1 all-gather.13
  323.6 27.2 reduce-scatter.7
